TPU v7x, 32 devices: a whole 2x2x4 slice. The times are simulated.
32 devices in a mesh: gx: 2 (over y), gy: 4 (over x, core), gz: 4 (over z).
Axes of the slice: x: 2, y: 2, z: 4, core: 2. Of those that a mesh axis runs over, the one named last changes fastest.
Arguments:
- loads: float32 [16, 4, 16, 1024], P(None, 'gx', 'gy', 'gz'), may hold values from -60 to 60
- moduli: float32 [8], replicated, may hold values from 0.5 to 4
- material: int32 [4, 16, 1024], P('gx', 'gy', 'gz'), may hold values from 0 to 7
Outputs:
- solution: float32 [16, 4, 16, 1024], P(None, 'gx', 'gy', 'gz')
- residual: float32 [16, 4, 16, 1024], P(None, 'gx', 'gy', 'gz')
All inputs are finite; a program needn't handle non-finite values.
Results may differ from a plain program's by a relative error of at most 0.005.
The roundings to bfloat16 on the way count: a program that leaves them out, or rounds other values in their place, can miss the bound.
Values may be sent and summed in bfloat16 or wider, within the bound.
A program may use at most 64 MiB of HBM per device.

v0:
```python
import jax
import jax.numpy as jnp
import numpy as np
from jax import lax
from jax.sharding import PartitionSpec as P

ITERS = 2


SIGMA = 0.25


def padded_2(cells, sides, width):
    for axis, dim in sides:
        count = lax.axis_size(axis)
        ends = count - 1
        head = lax.slice_in_dim(cells, 0, width, axis=dim)
        tail = lax.slice_in_dim(cells, cells.shape[dim] - width, cells.shape[dim], axis=dim)
        cells = jnp.concatenate(
            [
                lax.ppermute(tail, axis, [(i, (i + 1) % count) for i in range(ends)]),
                cells,
                lax.ppermute(head, axis, [((i + 1) % count, i) for i in range(ends)]),
            ],
            axis=dim,
        )
    return cells


def stiffness_table():
    line_mass = np.array([[1.0 / 3.0, 1.0 / 6.0], [1.0 / 6.0, 1.0 / 3.0]])
    line_stiff = np.array([[1.0, -1.0], [-1.0, 1.0]])
    table = np.zeros((8, 8))
    for target in range(8):
        for source in range(8):
            target_bits = [target >> 2 & 1, target >> 1 & 1, target & 1]
            source_bits = [source >> 2 & 1, source >> 1 & 1, source & 1]
            total = 0.0
            for stiff_dim in range(3):
                factor = 1.0
                for other in range(3):
                    if other == stiff_dim:
                        factor = factor * line_stiff[target_bits[other], source_bits[other]]
                    else:
                        factor = factor * line_mass[target_bits[other], source_bits[other]]
                total = total + factor
            table[target, source] = total
    return table


def corner_bits(corner):
    return (corner >> 2 & 1, corner >> 1 & 1, corner & 1)


def apply_operator(field, weights, kernel):
    lowered = field.astype(jnp.bfloat16)
    padded = padded_2(lowered, (("gx", 1), ("gy", 2), ("gz", 3)), 1)
    size_x, size_y, size_z = (field.shape[1], field.shape[2], field.shape[3])
    pieces = []
    for corner in range(8):
        bit_x, bit_y, bit_z = corner_bits(corner)
        pieces.append(
            padded[
                :,
                bit_x : bit_x + size_x + 1,
                bit_y : bit_y + size_y + 1,
                bit_z : bit_z + size_z + 1,
            ]
        )
    stacked = jnp.stack(pieces)
    total = SIGMA * field
    for corner in range(8):
        bit_x, bit_y, bit_z = corner_bits(corner)
        part = (
            jnp.einsum("b,bcxyz->cxyz", kernel[corner], stacked, preferred_element_type=jnp.float32)
            * weights
        )
        total = (
            total
            + part[
                :,
                1 - bit_x : 1 - bit_x + size_x,
                1 - bit_y : 1 - bit_y + size_y,
                1 - bit_z : 1 - bit_z + size_z,
            ]
        )
    return total


def local_gram(left, right):
    return jnp.einsum("cxyz,dxyz->cd", left, right, precision=lax.Precision.HIGHEST)


def combine(block, coeffs):
    return jnp.einsum("cxyz,cd->dxyz", block, coeffs, precision=lax.Precision.HIGHEST)


def solve_small(matrix, rhs_small):
    factor = jnp.linalg.cholesky(matrix)
    return jax.scipy.linalg.cho_solve((factor, True), rhs_small)


def residual_gram(residual):
    return lax.psum(local_gram(residual, residual), ("gx", "gy", "gz"))


def on_device(loads, moduli, material):
    kernel = jnp.asarray(stiffness_table(), jnp.float32).astype(jnp.bfloat16)
    levels = jnp.arange(moduli.shape[0], dtype=jnp.int32)
    node_modulus = jnp.sum(jnp.where(material[..., None] == levels, moduli, 0.0), axis=-1)
    padded_mod = padded_2(node_modulus, (("gx", 0), ("gy", 1), ("gz", 2)), 1)
    size_x, size_y, size_z = material.shape
    weights = jnp.zeros((size_x + 1, size_y + 1, size_z + 1), jnp.float32)
    for corner in range(8):
        bit_x, bit_y, bit_z = corner_bits(corner)
        weights = (
            weights
            + padded_mod[
                bit_x : bit_x + size_x + 1, bit_y : bit_y + size_y + 1, bit_z : bit_z + size_z + 1
            ]
        )
    weights = weights * 0.125
    solution = jnp.zeros_like(loads)
    residual = loads
    direction = loads
    current = residual_gram(residual)
    for iteration in range(ITERS):
        image = apply_operator(direction, weights, kernel)
        curvature, cross, image_sq = lax.psum(
            (local_gram(direction, image), local_gram(image, residual), local_gram(image, image)),
            ("gx", "gy", "gz"),
        )
        alpha = solve_small(curvature, current)
        solution = solution + combine(direction, alpha)
        residual = residual - combine(image, alpha)
        if iteration + 1 < ITERS:
            high = lax.Precision.HIGHEST
            cross_term = jnp.dot(alpha.T, cross, precision=high)
            quad_term = jnp.dot(jnp.dot(alpha.T, image_sq, precision=high), alpha, precision=high)
            updated = current - cross_term - cross_term.T + quad_term
            beta = solve_small(current, updated)
            direction = residual + combine(direction, beta)
            current = updated
    return (solution, residual)


def solution(mesh):
    in_specs = (P(None, "gx", "gy", "gz"), P(), P("gx", "gy", "gz"))
    out_specs = (P(None, "gx", "gy", "gz"), P(None, "gx", "gy", "gz"))
    return jax.shard_map(
        on_device, mesh=mesh, in_specs=in_specs, out_specs=out_specs, check_vma=False
    )
```

profile of v0, /device:TPU:0, one launch (start us, length us, event | category | flops | bytes accessed | tf_op | source)
XLA Modules:
  0.0 185.7 jit_solution(12359744168205889732)
XLA Ops:
  1.4 4.9 %collective-permute-start.6 = (f32[1,4,256]{2,1,0:T(4,128)S(1)}, f32[1,4,256]{2,1,0:T(4,128)S(1)}, u32[]{:S(2)}, u32[]{:S(2)}) collective-permute-start(f32[1,4,256]{2,1,0:T(4,128)S(1)} %get-tuple-element.42), channel_id=1, source_target_pairs={{0,16},{1,17},{2,18},{3,19},{4,20},{5,21},{6,22},{7,23},{8,24},{9,... | collective-permute-start | bytes 12296 | tf_op jit(solution)/shard_map/ppermute | solution.py:21
  6.4 1.3 collective-permute-start.7
  8.6 4.5 %collective-permute-start = (bf16[16,1,4,256]{3,2,1,0:T(4,128)(2,1)S(1)}, bf16[16,1,4,256]{3,2,1,0:T(4,128)(2,1)S(1)}, u32[]{:S(2)}, u32[]{:S(2)}) collective-permute-start(bf16[16,1,4,256]{3,2,1,0:T(4,128)(2,1)S(1)} %get-tuple-element.26), channel_id=1, source_target_pairs={{0,16},{1,17},{2,18},{3,19},{4,20},{5,21},{6,22},{7,23},{8,24},{9,... | collective-permute-start | bytes 98312 | tf_op jit(solution)/shard_map/ppermute | solution.py:21
  13.2 1.3 collective-permute-start.1
  14.5 1.3 collective-permute-start.8
  15.8 1.3 collective-permute-start.9
  17.1 1.3 convolution_bitcast_fusion.4
  18.4 2.2 %collective-permute-done.9 = f32[4,1,256]{2,1,0:T(1,128)S(1)} collective-permute-done((f32[4,1,256]{2,1,0:T(1,128)S(1)}, f32[4,1,256]{2,1,0:T(1,128)S(1)}, u32[]{:S(2)}, u32[]{:S(2)}) %collective-permute-start.9) | collective-permute-done | bytes 4128 | tf_op jit(solution)/shard_map/ppermute | solution.py:23
  20.7 3.5 %collective-permute-start.10 = (f32[4,6,1]{2,1,0:T(8,128)S(1)}, f32[4,6,1]{2,1,0:T(8,128)S(1)}, u32[]{:S(2)}, u32[]{:S(2)}) collective-permute-start(f32[4,6,1]{2,1,0:T(8,128)S(1)} %get-tuple-element.36), channel_id=1, source_target_pairs={{0,1},{1,2},{2,3},{4,5},{5,6},{6,7},{8,9},{9,10},{10,11},{12,13},{... | collective-permute-start | bytes 296 | tf_op jit(solution)/shard_map/ppermute | solution.py:21
  24.2 1.3 collective-permute-start.11
  25.6 4.2 %collective-permute-done.11 = f32[4,6,1]{2,1,0:T(8,128)S(1)} collective-permute-done((f32[4,6,1]{2,1,0:T(8,128)S(1)}, f32[4,6,1]{2,1,0:T(8,128)S(1)}, u32[]{:S(2)}, u32[]{:S(2)}) %collective-permute-start.11) | collective-permute-done | bytes 128 | tf_op jit(solution)/shard_map/ppermute | solution.py:23
  30.1 2.8 %collective-permute-start.2 = (bf16[16,4,1,256]{3,2,1,0:T(2,128)(2,1)S(1)}, bf16[16,4,1,256]{3,2,1,0:T(2,128)(2,1)S(1)}, u32[]{:S(2)}, u32[]{:S(2)}) collective-permute-start(bf16[16,4,1,256]{3,2,1,0:T(2,128)(2,1)S(1)} %get-tuple-element.22), channel_id=1, source_target_pairs={{0,4},{4,8},{8,12},{1,5},{5,9},{9,13},{2,6},{6,10},{10,14},{3,7},{... | collective-permute-start | bytes 98312 | tf_op jit(solution)/shard_map/ppermute | solution.py:21
  33.0 1.3 collective-permute-start.3
  34.3 2.8 %collective-permute-done.3 = bf16[16,4,1,256]{3,2,1,0:T(2,128)(2,1)S(1)} collective-permute-done((bf16[16,4,1,256]{3,2,1,0:T(2,128)(2,1)S(1)}, bf16[16,4,1,256]{3,2,1,0:T(2,128)(2,1)S(1)}, u32[]{:S(2)}, u32[]{:S(2)}) %collective-permute-start.3) | collective-permute-done | bytes 32800 | tf_op jit(solution)/shard_map/ppermute | solution.py:23
  37.5 3.5 %collective-permute-start.4 = (bf16[16,4,6,1]{3,2,1,0:T(8,128)(2,1)S(1)}, bf16[16,4,6,1]{3,2,1,0:T(8,128)(2,1)S(1)}, u32[]{:S(2)}, u32[]{:S(2)}) collective-permute-start(bf16[16,4,6,1]{3,2,1,0:T(8,128)(2,1)S(1)} %get-tuple-element.15), channel_id=1, source_target_pairs={{0,1},{1,2},{2,3},{4,5},{5,6},{6,7},{8,9},{9,10},{10,11},{12,13},{... | collective-permute-start | bytes 2312 | tf_op jit(solution)/shard_map/ppermute | solution.py:21
  41.0 1.3 collective-permute-start.5
  43.5 4.4 %collective-permute-done.5 = bf16[16,4,6,1]{3,2,1,0:T(8,128)(2,1)S(1)} collective-permute-done((bf16[16,4,6,1]{3,2,1,0:T(8,128)(2,1)S(1)}, bf16[16,4,6,1]{3,2,1,0:T(8,128)(2,1)S(1)}, u32[]{:S(2)}, u32[]{:S(2)}) %collective-permute-start.5) | collective-permute-done | bytes 800 | tf_op jit(solution)/shard_map/ppermute | solution.py:23
  49.3 1.6 copy.46
  57.3 43.2 %all-reduce = (f32[16,16]{0,1:T(8,128)S(1)}, f32[16,16]{0,1:T(8,128)S(1)}, f32[16,16]{1,0:T(8,128)S(1)}, f32[16,16]{1,0:T(8,128)S(1)}) all-reduce(f32[16,16]{0,1:T(8,128)S(1)} %convolution_bitcast_fusion.4, f32[16,16]{0,1:T(8,128)S(1)} %bitcast.265, ...), channel_id=1, replica_groups=mesh['gx'=2,'gy'=4,'gz'=4] {'gx','gy','gz'}, use_global_device_ids=true, to_apply=%region_4.0 | all-reduce | flops 1024 | bytes 8192 | tf_op jit(solution)/shard_map/psum | solution.py:104
  100.6 1.5 cholesky.70
  104.7 1.5 cholesky.59
  110.8 4.2 %collective-permute-start.12 = (bf16[16,1,4,256]{3,0,2,1:T(8,128)(2,1)S(1)}, bf16[16,1,4,256]{3,0,2,1:T(8,128)(2,1)S(1)}, u32[]{:S(2)}, u32[]{:S(2)}) collective-permute-start(bf16[16,1,4,256]{3,0,2,1:T(8,128)(2,1)S(1)} %get-tuple-element.24), channel_id=1, source_target_pairs={{0,16},{1,17},{2,18},{3,19},{4,20},{5,21},{6,22},{7,23},{8,24},{9,... | collective-permute-start | bytes 98312 | tf_op jit(solution)/shard_map/ppermute | solution.py:21
  115.0 1.3 collective-permute-start.13
  116.6 4.2 %collective-permute-done.13 = bf16[16,1,4,256]{3,0,2,1:T(8,128)(2,1)S(1)} collective-permute-done((bf16[16,1,4,256]{3,0,2,1:T(8,128)(2,1)S(1)}, bf16[16,1,4,256]{3,0,2,1:T(8,128)(2,1)S(1)}, u32[]{:S(2)}, u32[]{:S(2)}) %collective-permute-start.13) | collective-permute-done | bytes 32800 | tf_op jit(solution)/shard_map/ppermute | solution.py:23
  120.8 1.3 collective-permute-start.14
  122.1 1.3 collective-permute-start.15
  123.5 2.1 %collective-permute-done.15 = bf16[16,4,1,256]{3,0,2,1:T(8,128)(2,1)S(1)} collective-permute-done((bf16[16,4,1,256]{3,0,2,1:T(8,128)(2,1)S(1)}, bf16[16,4,1,256]{3,0,2,1:T(8,128)(2,1)S(1)}, u32[]{:S(2)}, u32[]{:S(2)}) %collective-permute-start.15) | collective-permute-done | bytes 32800 | tf_op jit(solution)/shard_map/ppermute | solution.py:23
  125.7 2.3 %collective-permute-start.16 = (bf16[16,4,6,1]{3,0,2,1:T(8,128)(2,1)S(1)}, bf16[16,4,6,1]{3,0,2,1:T(8,128)(2,1)S(1)}, u32[]{:S(2)}, u32[]{:S(2)}) collective-permute-start(bf16[16,4,6,1]{3,0,2,1:T(8,128)(2,1)S(1)} %get-tuple-element.19), channel_id=1, source_target_pairs={{0,1},{1,2},{2,3},{4,5},{5,6},{6,7},{8,9},{9,10},{10,11},{12,13},{... | collective-permute-start | bytes 2312 | tf_op jit(solution)/shard_map/ppermute | solution.py:21
  128.1 1.3 collective-permute-start.17
  130.3 4.3 %collective-permute-done.17 = bf16[16,4,6,1]{3,0,2,1:T(8,128)(2,1)S(1)} collective-permute-done((bf16[16,4,6,1]{3,0,2,1:T(8,128)(2,1)S(1)}, bf16[16,4,6,1]{3,0,2,1:T(8,128)(2,1)S(1)}, u32[]{:S(2)}, u32[]{:S(2)}) %collective-permute-start.17) | collective-permute-done | bytes 800 | tf_op jit(solution)/shard_map/ppermute | solution.py:23
  140.0 39.1 %psum.39 = f32[16,16]{0,1:T(8,128)S(1)} all-reduce(f32[16,16]{0,1:T(8,128)S(1)} %convolution_bitcast_fusion.1), channel_id=1, replica_groups=mesh['gx'=2,'gy'=4,'gz'=4] {'gx','gy','gz'}, use_global_device_ids=true, to_apply=%region_7.10 | all-reduce | flops 256 | bytes 2048 | tf_op jit(solution)/shard_map/psum | solution.py:129
  179.3 1.5 cholesky.81
  (133 shorter events, 30.4 us)
Async XLA Ops:
  1.4 13.0 %collective-permute-start.6 = (f32[1,4,256]{2,1,0:T(4,128)S(1)}, f32[1,4,256]{2,1,0:T(4,128)S(1)}, u32[]{:S(2)}, u32[]{:S(2)}) collective-permute-start(f32[1,4,256]{2,1,0:T(4,128)S(1)} %get-tuple-element.42), channel_id=1, source_target_pairs={{0,16},{1,17},{2,18},{3,19},{4,20},{5,21},{6,22},{7,23},{8,24},{9,... | collective-permute-start | bytes 12296 | tf_op jit(solution)/shard_map/ppermute | solution.py:21
  6.4 8.1 %collective-permute-start.7 = (f32[1,4,256]{2,1,0:T(4,128)S(1)}, f32[1,4,256]{2,1,0:T(4,128)S(1)}, u32[]{:S(2)}, u32[]{:S(2)}) collective-permute-start(f32[1,4,256]{2,1,0:T(4,128)S(1)} %get-tuple-element.43), channel_id=1, source_target_pairs={{16,0},{17,1},{18,2},{19,3},{20,4},{21,5},{22,6},{23,7},{24,8},{25... | collective-permute-start | bytes 12296 | tf_op jit(solution)/shard_map/ppermute | solution.py:23
  8.6 21.3 %collective-permute-start = (bf16[16,1,4,256]{3,2,1,0:T(4,128)(2,1)S(1)}, bf16[16,1,4,256]{3,2,1,0:T(4,128)(2,1)S(1)}, u32[]{:S(2)}, u32[]{:S(2)}) collective-permute-start(bf16[16,1,4,256]{3,2,1,0:T(4,128)(2,1)S(1)} %get-tuple-element.26), channel_id=1, source_target_pairs={{0,16},{1,17},{2,18},{3,19},{4,20},{5,21},{6,22},{7,23},{8,24},{9,... | collective-permute-start | bytes 98312 | tf_op jit(solution)/shard_map/ppermute | solution.py:21
  13.2 16.8 %collective-permute-start.1 = (bf16[16,1,4,256]{3,2,1,0:T(4,128)(2,1)S(1)}, bf16[16,1,4,256]{3,2,1,0:T(4,128)(2,1)S(1)}, u32[]{:S(2)}, u32[]{:S(2)}) collective-permute-start(bf16[16,1,4,256]{3,2,1,0:T(4,128)(2,1)S(1)} %get-tuple-element.27), channel_id=1, source_target_pairs={{16,0},{17,1},{18,2},{19,3},{20,4},{21,5},{22,6},{23,7},{24,8},{25... | collective-permute-start | bytes 98312 | tf_op jit(solution)/shard_map/ppermute | solution.py:23
  14.5 3.9 %collective-permute-start.8 = (f32[4,1,256]{2,1,0:T(1,128)S(1)}, f32[4,1,256]{2,1,0:T(1,128)S(1)}, u32[]{:S(2)}, u32[]{:S(2)}) collective-permute-start(f32[4,1,256]{2,1,0:T(1,128)S(1)} %get-tuple-element.40), channel_id=1, source_target_pairs={{0,4},{4,8},{8,12},{1,5},{5,9},{9,13},{2,6},{6,10},{10,14},{3,7},{... | collective-permute-start | bytes 12296 | tf_op jit(solution)/shard_map/ppermute | solution.py:21
  15.8 4.8 %collective-permute-start.9 = (f32[4,1,256]{2,1,0:T(1,128)S(1)}, f32[4,1,256]{2,1,0:T(1,128)S(1)}, u32[]{:S(2)}, u32[]{:S(2)}) collective-permute-start(f32[4,1,256]{2,1,0:T(1,128)S(1)} %get-tuple-element.41), channel_id=1, source_target_pairs={{4,0},{8,4},{12,8},{5,1},{9,5},{13,9},{6,2},{10,6},{14,10},{7,3},{... | collective-permute-start | bytes 12296 | tf_op jit(solution)/shard_map/ppermute | solution.py:23
  20.7 4.9 %collective-permute-start.10 = (f32[4,6,1]{2,1,0:T(8,128)S(1)}, f32[4,6,1]{2,1,0:T(8,128)S(1)}, u32[]{:S(2)}, u32[]{:S(2)}) collective-permute-start(f32[4,6,1]{2,1,0:T(8,128)S(1)} %get-tuple-element.36), channel_id=1, source_target_pairs={{0,1},{1,2},{2,3},{4,5},{5,6},{6,7},{8,9},{9,10},{10,11},{12,13},{... | collective-permute-start | bytes 296 | tf_op jit(solution)/shard_map/ppermute | solution.py:21
  24.2 5.6 %collective-permute-start.11 = (f32[4,6,1]{2,1,0:T(8,128)S(1)}, f32[4,6,1]{2,1,0:T(8,128)S(1)}, u32[]{:S(2)}, u32[]{:S(2)}) collective-permute-start(f32[4,6,1]{2,1,0:T(8,128)S(1)} %get-tuple-element.37), channel_id=1, source_target_pairs={{1,0},{2,1},{3,2},{5,4},{6,5},{7,6},{9,8},{10,9},{11,10},{13,12},{... | collective-permute-start | bytes 296 | tf_op jit(solution)/shard_map/ppermute | solution.py:23
  30.1 4.2 %collective-permute-start.2 = (bf16[16,4,1,256]{3,2,1,0:T(2,128)(2,1)S(1)}, bf16[16,4,1,256]{3,2,1,0:T(2,128)(2,1)S(1)}, u32[]{:S(2)}, u32[]{:S(2)}) collective-permute-start(bf16[16,4,1,256]{3,2,1,0:T(2,128)(2,1)S(1)} %get-tuple-element.22), channel_id=1, source_target_pairs={{0,4},{4,8},{8,12},{1,5},{5,9},{9,13},{2,6},{6,10},{10,14},{3,7},{... | collective-permute-start | bytes 98312 | tf_op jit(solution)/shard_map/ppermute | solution.py:21
  33.0 4.2 %collective-permute-start.3 = (bf16[16,4,1,256]{3,2,1,0:T(2,128)(2,1)S(1)}, bf16[16,4,1,256]{3,2,1,0:T(2,128)(2,1)S(1)}, u32[]{:S(2)}, u32[]{:S(2)}) collective-permute-start(bf16[16,4,1,256]{3,2,1,0:T(2,128)(2,1)S(1)} %get-tuple-element.23), channel_id=1, source_target_pairs={{4,0},{8,4},{12,8},{5,1},{9,5},{13,9},{6,2},{10,6},{14,10},{7,3},{... | collective-permute-start | bytes 98312 | tf_op jit(solution)/shard_map/ppermute | solution.py:23
  37.5 6.0 %collective-permute-start.4 = (bf16[16,4,6,1]{3,2,1,0:T(8,128)(2,1)S(1)}, bf16[16,4,6,1]{3,2,1,0:T(8,128)(2,1)S(1)}, u32[]{:S(2)}, u32[]{:S(2)}) collective-permute-start(bf16[16,4,6,1]{3,2,1,0:T(8,128)(2,1)S(1)} %get-tuple-element.15), channel_id=1, source_target_pairs={{0,1},{1,2},{2,3},{4,5},{5,6},{6,7},{8,9},{9,10},{10,11},{12,13},{... | collective-permute-start | bytes 2312 | tf_op jit(solution)/shard_map/ppermute | solution.py:21
  41.0 6.9 %collective-permute-start.5 = (bf16[16,4,6,1]{3,2,1,0:T(8,128)(2,1)S(1)}, bf16[16,4,6,1]{3,2,1,0:T(8,128)(2,1)S(1)}, u32[]{:S(2)}, u32[]{:S(2)}) collective-permute-start(bf16[16,4,6,1]{3,2,1,0:T(8,128)(2,1)S(1)} %get-tuple-element.14), channel_id=1, source_target_pairs={{1,0},{2,1},{3,2},{5,4},{6,5},{7,6},{9,8},{10,9},{11,10},{13,12},{... | collective-permute-start | bytes 2312 | tf_op jit(solution)/shard_map/ppermute | solution.py:23
  49.3 1.6 copy-start.1
  51.0 0.7 copy-start.2
  51.0 1.2 copy-start.3
  51.6 1.1 copy-start.4
  52.2 1.1 copy-start.5
  52.7 1.1 copy-start.6
  53.3 1.1 copy-start.7
  53.8 1.1 copy-start.8
  55.6 0.9 copy-start
  110.8 5.8 %collective-permute-start.12 = (bf16[16,1,4,256]{3,0,2,1:T(8,128)(2,1)S(1)}, bf16[16,1,4,256]{3,0,2,1:T(8,128)(2,1)S(1)}, u32[]{:S(2)}, u32[]{:S(2)}) collective-permute-start(bf16[16,1,4,256]{3,0,2,1:T(8,128)(2,1)S(1)} %get-tuple-element.24), channel_id=1, source_target_pairs={{0,16},{1,17},{2,18},{3,19},{4,20},{5,21},{6,22},{7,23},{8,24},{9,... | collective-permute-start | bytes 98312 | tf_op jit(solution)/shard_map/ppermute | solution.py:21
  115.0 5.8 %collective-permute-start.13 = (bf16[16,1,4,256]{3,0,2,1:T(8,128)(2,1)S(1)}, bf16[16,1,4,256]{3,0,2,1:T(8,128)(2,1)S(1)}, u32[]{:S(2)}, u32[]{:S(2)}) collective-permute-start(bf16[16,1,4,256]{3,0,2,1:T(8,128)(2,1)S(1)} %get-tuple-element.25), channel_id=1, source_target_pairs={{16,0},{17,1},{18,2},{19,3},{20,4},{21,5},{22,6},{23,7},{24,8},{25... | collective-permute-start | bytes 98312 | tf_op jit(solution)/shard_map/ppermute | solution.py:23
  120.8 2.6 %collective-permute-start.14 = (bf16[16,4,1,256]{3,0,2,1:T(8,128)(2,1)S(1)}, bf16[16,4,1,256]{3,0,2,1:T(8,128)(2,1)S(1)}, u32[]{:S(2)}, u32[]{:S(2)}) collective-permute-start(bf16[16,4,1,256]{3,0,2,1:T(8,128)(2,1)S(1)} %get-tuple-element.20), channel_id=1, source_target_pairs={{0,4},{4,8},{8,12},{1,5},{5,9},{9,13},{2,6},{6,10},{10,14},{3,7},{... | collective-permute-start | bytes 98312 | tf_op jit(solution)/shard_map/ppermute | solution.py:21
  122.1 3.5 %collective-permute-start.15 = (bf16[16,4,1,256]{3,0,2,1:T(8,128)(2,1)S(1)}, bf16[16,4,1,256]{3,0,2,1:T(8,128)(2,1)S(1)}, u32[]{:S(2)}, u32[]{:S(2)}) collective-permute-start(bf16[16,4,1,256]{3,0,2,1:T(8,128)(2,1)S(1)} %get-tuple-element.21), channel_id=1, source_target_pairs={{4,0},{8,4},{12,8},{5,1},{9,5},{13,9},{6,2},{10,6},{14,10},{7,3},{... | collective-permute-start | bytes 98312 | tf_op jit(solution)/shard_map/ppermute | solution.py:23
  125.7 4.5 %collective-permute-start.16 = (bf16[16,4,6,1]{3,0,2,1:T(8,128)(2,1)S(1)}, bf16[16,4,6,1]{3,0,2,1:T(8,128)(2,1)S(1)}, u32[]{:S(2)}, u32[]{:S(2)}) collective-permute-start(bf16[16,4,6,1]{3,0,2,1:T(8,128)(2,1)S(1)} %get-tuple-element.19), channel_id=1, source_target_pairs={{0,1},{1,2},{2,3},{4,5},{5,6},{6,7},{8,9},{9,10},{10,11},{12,13},{... | collective-permute-start | bytes 2312 | tf_op jit(solution)/shard_map/ppermute | solution.py:21
  128.1 6.5 %collective-permute-start.17 = (bf16[16,4,6,1]{3,0,2,1:T(8,128)(2,1)S(1)}, bf16[16,4,6,1]{3,0,2,1:T(8,128)(2,1)S(1)}, u32[]{:S(2)}, u32[]{:S(2)}) collective-permute-start(bf16[16,4,6,1]{3,0,2,1:T(8,128)(2,1)S(1)} %get-tuple-element.18), channel_id=1, source_target_pairs={{1,0},{2,1},{3,2},{5,4},{6,5},{7,6},{9,8},{10,9},{11,10},{13,12},{... | collective-permute-start | bytes 2312 | tf_op jit(solution)/shard_map/ppermute | solution.py:23
where the time goes:
time: 187 us; the launch traced here: 186 us
  blocking collectives  82.4 us (44%)
  starting transfers between devices  40 us (21%)
  waiting for transfers between devices  26.4 us (14%)
  other arithmetic  15.8 us (8%)
  matrix products  13.6 us (7%)
  local copies, waits for them, and re-layouts  6.08 us (3%)
    psum x1, blocking collectives, residual_gram(): return lax.psum(local_gram(residual, residual), ('gx', 'gy', 'gz'))  43.2 us
    psum x1, blocking collectives, on_device(): lax.psum((local_gram(direction, image), local_gram(image, residual), loca...  39.1 us
    ppermute x9, starting transfers between devices, padded_2(): lax.ppermute(tail, axis, [(i, (i + 1) % count) for i in range(ends)])  28.4 us
    ppermute x9, waiting for transfers between devices, padded_2(): lax.ppermute(head, axis, [((i + 1) % count, i) for i in range(ends)])  24.2 us
    ppermute x9, starting transfers between devices, padded_2(): lax.ppermute(head, axis, [((i + 1) % count, i) for i in range(ends)])  11.6 us
    dot_general x16, matrix products, apply_operator(): jnp.einsum('b,bcxyz->cxyz', kernel[corner], stacked, preferred_element_ty...  8.36 us
    another operation x9, other arithmetic, solve_small(): factor = jnp.linalg.cholesky(matrix)  6.4 us
    another operation x6, other arithmetic, solve_small(): return jax.scipy.linalg.cho_solve((factor, True), rhs_small)  5.63 us
  transfers between devices with their start and end apart: 18, of which 12 were waited for; matrix products, arithmetic and copies ran while one was open for 2% of the time, Pallas kernels for 0%

commit v1 on v0

v1 whole, which is shorter than its diff:
```python
import functools
import itertools

import jax
import jax.numpy as jnp
import numpy as np
from jax import lax
from jax.experimental import pallas as pl
from jax.experimental.pallas import tpu as pltpu
from jax.sharding import PartitionSpec as P

SIGMA = 0.25
AXES = ("gx", "gy", "gz")
HIGH = lax.Precision.HIGHEST
F32 = jnp.float32
BF16 = jnp.bfloat16
LANES = 128
DIRECT_LIMIT = 32


def stiffness_values():
    mass = (1.0 / 3.0, 1.0 / 6.0)
    stiff = (1.0, -1.0)
    values = []
    for differing in range(4):
        bits = [1 if dim < differing else 0 for dim in range(3)]
        total = 0.0
        for dim in range(3):
            factor = 1.0
            for other in range(3):
                factor *= stiff[bits[other]] if other == dim else mass[bits[other]]
            total += factor
        values.append(float(np.asarray(total, np.float32).astype(jnp.bfloat16).astype(np.float32)))
    return values


def dot(left, right, left_dim, right_dim, precision=HIGH):
    return lax.dot_general(
        left, right, (((left_dim,), (right_dim,)), ((), ())), precision=precision, preferred_element_type=F32
    )


def pack(matrix):
    rows = matrix.shape[0]
    wide = jnp.concatenate([matrix, jnp.zeros((rows, LANES - matrix.shape[1]), F32)], axis=1)
    tile = wide[0:8]
    for group in range(1, rows // 8):
        tile = tile + pltpu.roll(wide[8 * group : 8 * group + 8], 32 * group, 1)
    return tile


def unpack(tile):
    pieces = [tile] + [pltpu.roll(tile, LANES - 32 * group, 1) for group in range(1, 4)]
    return jnp.concatenate(pieces, axis=0)[:, 0:32]


def eliminate(matrix, rhs):
    size = matrix.shape[0]
    both = jnp.concatenate([matrix, rhs], axis=1)
    rows = lax.broadcasted_iota(jnp.int32, both.shape, 0)
    for step in range(size):
        pivot_row = both[step : step + 1, :]
        scaled = pivot_row / pivot_row[:, step : step + 1]
        column = both[:, step : step + 1]
        both = jnp.where(rows == step, scaled, both - column * scaled)
    return both[:, size:]


def kernel_body(sizes, phases, stiff, moduli_ref, loads_ref, mat_ref, sol_ref, res_ref,
                stack, padded, sides, padded_im, sides_im, field, wt, wtr, stack2, shares,
                halo_send, halo_recv, sum_send, sum_recv):
    cols = loads_ref.shape[2]
    nx, ny, nz = loads_ref.shape[0], loads_ref.shape[1], loads_ref.shape[3]
    mats = moduli_ref.shape[0]
    me = [lax.axis_index(axis) for axis in AXES]
    k_self, k_edge, k_far = stiff[0], stiff[1], stiff[2]
    assert k_edge == 0.0 and stiff[2] == stiff[3]
    xs, ys = range(nx + 2), range(ny + 2)
    own = list(itertools.product(range(nx), range(ny)))

    directions = [
        d for d in itertools.product((-1, 0, 1), repeat=3)
        if any(d) and all(step == 0 or sizes[i] > 1 for i, step in enumerate(d))
    ]

    def exists(direction):
        good = None
        for i, step in enumerate(direction):
            if step:
                here = (me[i] > 0) if step < 0 else (me[i] < sizes[i] - 1)
                good = here if good is None else jnp.logical_and(good, here)
        return good

    def target(direction):
        return {axis: me[i] + direction[i] for i, axis in enumerate(AXES)}

    def halo_copy(round_, number, core, edge):
        dx, dy, dz = directions[number]
        src_x = {0: pl.ds(1, nx), 1: pl.ds(nx, 1), -1: pl.ds(1, 1)}[dx]
        dst_x = {0: pl.ds(1, nx), 1: pl.ds(0, 1), -1: pl.ds(nx + 1, 1)}[dx]
        src_y = {0: pl.ds(1, ny), 1: pl.ds(ny, 1), -1: pl.ds(1, 1)}[dy]
        dst_y = {0: pl.ds(1, ny), 1: pl.ds(0, 1), -1: pl.ds(ny + 1, 1)}[dy]
        if dz == 0:
            src, dst = core.at[src_x, src_y], core.at[dst_x, dst_y]
        else:
            start = nz - LANES if dz > 0 else 0
            src = core.at[src_x, src_y, :, pl.ds(start, LANES)]
            dst = edge.at[0 if dz > 0 else 1, dst_x, dst_y]
        return pltpu.make_async_remote_copy(
            src_ref=src, dst_ref=dst, send_sem=halo_send.at[round_, number], recv_sem=halo_recv.at[round_, number],
            device_id=target((dx, dy, dz)), device_id_type=pl.DeviceIdType.MESH,
        )

    def halo_start(round_, core, edge):
        for number, direction in enumerate(directions):
            @pl.when(exists(direction))
            def _():
                halo_copy(round_, number, core, edge).start()

    def halo_arrive(round_, core, edge):
        for number, direction in enumerate(directions):
            @pl.when(exists(tuple(-step for step in direction)))
            def _():
                halo_copy(round_, number, core, edge).wait_recv()

    def halo_left(round_, core, edge):
        for number, direction in enumerate(directions):
            @pl.when(exists(direction))
            def _():
                halo_copy(round_, number, core, edge).wait_send()

    def group_of(axes):
        count, index = 1, 0
        for axis in axes:
            i = AXES.index(axis)
            count *= sizes[i]
            index = index * sizes[i] + me[i]
        return count, index

    def peer_id(axes, peer):
        coords = {axis: me[i] for i, axis in enumerate(AXES)}
        for axis in reversed(axes):
            size = sizes[AXES.index(axis)]
            coords[axis] = lax.rem(peer, size)
            peer = lax.div(peer, size)
        return coords

    offsets = []
    total_slots = 0
    for axes in phases:
        offsets.append(total_slots)
        total_slots += group_of(axes)[0]

    for x in xs:
        for y in ys:
            padded[x, y] = jnp.zeros(padded.shape[2:], BF16)
            padded_im[x, y] = jnp.zeros(padded_im.shape[2:], BF16)
            for side in range(2):
                sides[side, x, y] = jnp.zeros(sides.shape[3:], BF16)
                sides_im[side, x, y] = jnp.zeros(sides_im.shape[3:], BF16)

    barrier = pltpu.get_barrier_semaphore()
    expected = 0
    for axes in phases:
        count, index = group_of(axes)

        def greet(k, carry, axes=axes, count=count, index=index):
            pl.semaphore_signal(barrier, inc=1, device_id=peer_id(axes, lax.rem(index + k, count)),
                                device_id_type=pl.DeviceIdType.MESH)
            return carry

        lax.fori_loop(1, count, greet, 0)
        expected = expected + count - 1
    if len(phases) > 1:
        for direction in directions:
            good = exists(direction)

            @pl.when(good)
            def _():
                pl.semaphore_signal(barrier, inc=1, device_id=target(direction),
                                    device_id_type=pl.DeviceIdType.MESH)
            expected = expected + jnp.where(good, 1, 0)

    for x, y in own:
        values = loads_ref[x, y]
        stack[x, y, 0:cols, :] = values
        padded[x + 1, y + 1, 0:cols, :] = values.astype(BF16)
        row = x * ny + y
        ids = (mat_ref[row : row + 1, :] + 1).astype(F32)
        padded[x + 1, y + 1, cols:, :] = jnp.broadcast_to(ids, (cols, nz)).astype(BF16)
    pl.semaphore_wait(barrier, expected)
    halo_start(0, padded, sides)
    halo_arrive(0, padded, sides)

    lane = lax.broadcasted_iota(jnp.int32, (1, LANES), 1)

    def merged(edge, x, y):
        left, right = edge[0, x, y].astype(F32), edge[1, x, y].astype(F32)
        return jnp.where(lane == 0, right, jnp.where(lane == LANES - 1, left, 0.0))

    full = nz + LANES
    moduli = {}
    for x in xs:
        for y in ys:
            tail = merged(sides, x, y)
            everything = jnp.concatenate([padded[x, y].astype(F32), tail], axis=1)
            field[x, y] = everything[0:cols]
            ids = everything[cols : cols + 8]
            modulus = jnp.zeros_like(ids)
            for number in range(mats):
                modulus = modulus + jnp.where(ids == float(number + 1), moduli_ref[number], 0.0)
            moduli[x, y] = modulus
    for x in range(nx + 1):
        for y in range(ny + 1):
            total = (moduli[x, y] + moduli[x, y + 1]) + (moduli[x + 1, y] + moduli[x + 1, y + 1])
            weight = 0.125 * (total + pltpu.roll(total, full - 1, 1))
            wt[x, y] = weight
            wtr[x, y] = pltpu.roll(weight, 1, 1)

    def double(tile):
        return jnp.concatenate([tile, tile], axis=0)

    def operate(direction_of, write):
        for x in range(nx):
            for y in range(ny):
                here = field[x + 1, y + 1]
                ahead = behind = flat = None
                w_ahead = w_behind = None
                for ex in (x, x + 1):
                    for ey in (y, y + 1):
                        corner_sum = (field[ex, ey] + field[ex, ey + 1]) + (field[ex + 1, ey] + field[ex + 1, ey + 1])
                        after, before = wt[ex, ey], wtr[ex, ey]
                        opposite = field[2 * ex - x, 2 * ey - y][:, 0:nz]
                        one = double(before) * corner_sum
                        two = double(after) * corner_sum
                        three = double((before + after)[:, 0:nz]) * opposite
                        ahead = one if ahead is None else ahead + one
                        behind = two if behind is None else behind + two
                        flat = three if flat is None else flat + three
                        w_ahead = before if w_ahead is None else w_ahead + before
                        w_behind = after if w_behind is None else w_behind + after
                ahead = ahead - double(w_ahead) * here
                behind = behind - double(w_behind) * here
                around = pltpu.roll(ahead, full - 1, 1)[:, 0:nz] + pltpu.roll(behind, 1, 1)[:, 0:nz] + flat
                centre = double((w_ahead + w_behind)[:, 0:nz]) * here[:, 0:nz]
                write(x, y, SIGMA * direction_of(x, y) + (k_far * around + k_self * centre))

    def gram(block):
        total = None
        for x, y in own:
            part = dot(block[x, y], block[x, y], 1, 1)
            total = part if total is None else total + part
        return total

    def sum_copy(round_, number, k):
        axes = phases[number]
        count, index = group_of(axes)
        slot = offsets[number] + index
        return pltpu.make_async_remote_copy(
            src_ref=shares.at[round_, slot], dst_ref=shares.at[round_, slot],
            send_sem=sum_send.at[round_, offsets[number] + k], recv_sem=sum_recv.at[round_, offsets[number] + k],
            device_id=peer_id(axes, lax.rem(index + k, count)), device_id_type=pl.DeviceIdType.MESH,
        )

    def sum_arrival(round_, number, k):
        axes = phases[number]
        count, index = group_of(axes)
        source = lax.rem(index + count - k, count)
        slot = offsets[number] + source
        return pltpu.make_async_remote_copy(
            src_ref=shares.at[round_, slot], dst_ref=shares.at[round_, slot],
            send_sem=sum_send.at[round_, offsets[number] + k], recv_sem=sum_recv.at[round_, offsets[number] + k],
            device_id=peer_id(axes, lax.rem(index + k, count)), device_id_type=pl.DeviceIdType.MESH,
        )

    def sum_start(round_, number, tile):
        count, index = group_of(phases[number])
        shares[round_, offsets[number] + index] = tile

        def send(k, carry):
            sum_copy(round_, number, k).start()
            return carry

        lax.fori_loop(1, count, send, 0)

    def sum_finish(round_, number):
        count, _ = group_of(phases[number])

        def receive(k, carry):
            sum_arrival(round_, number, k).wait_recv()
            return carry

        lax.fori_loop(1, count, receive, 0)
        tile = shares[round_, offsets[number]]
        for peer in range(1, count):
            tile = tile + shares[round_, offsets[number] + peer]
        return tile

    def sum_rest(round_):
        tile = sum_finish(round_, 0)
        for number in range(1, len(phases)):
            sum_start(round_, number, tile)
            tile = sum_finish(round_, number)
        return unpack(tile)

    def sum_left(round_):
        for number, axes in enumerate(phases):
            def drain(k, carry, number=number):
                sum_copy(round_, number, k).wait_send()
                return carry

            lax.fori_loop(1, group_of(axes)[0], drain, 0)

    def write_first(x, y, image):
        stack[x, y, cols:, :] = image
        padded_im[x + 1, y + 1] = image.astype(BF16)

    operate(lambda x, y: stack[x, y, 0:cols, :], write_first)
    sum_start(0, 0, pack(gram(stack)))
    halo_start(1, padded_im, sides_im)
    table = sum_rest(0)

    square = table[0:cols, 0:cols]
    curve = 0.5 * (table[0:cols, cols:] + table[cols:, 0:cols])
    row_id = lax.broadcasted_iota(jnp.int32, (cols, cols), 0)
    col_id = lax.broadcasted_iota(jnp.int32, (cols, cols), 1)
    eye = jnp.where(row_id == col_id, 1.0, 0.0)
    alpha = eliminate(curve, square)
    inverse = eliminate(square, eye)
    half = table[:, 0:cols] - dot(table[:, cols:], alpha, 1, 0)
    updated = half[0:cols] - dot(alpha, half[cols:], 0, 0)
    beta = dot(inverse, updated, 1, 0)
    alpha_t = alpha.T
    mix = jnp.concatenate([(eye + beta).T, -alpha_t], axis=1)
    mix_hi = mix.astype(BF16)
    mix_lo = (mix - mix_hi.astype(F32)).astype(BF16)
    mix_both = jnp.concatenate([mix_hi, mix_lo], axis=0)

    halo_arrive(1, padded_im, sides_im)
    for x in xs:
        for y in ys:
            inner = 1 <= x <= nx and 1 <= y <= ny
            tail_l = merged(sides, x, y)[0:cols].astype(BF16)
            tail_i = merged(sides_im, x, y).astype(BF16)
            if inner:
                near = jnp.concatenate([tail_l, tail_i], axis=0)
            else:
                near = jnp.concatenate([
                    jnp.concatenate([padded[x, y, 0:cols, :], tail_l], axis=1),
                    jnp.concatenate([padded_im[x, y], tail_i], axis=1),
                ], axis=0)
            twice = dot(mix_both, near, 1, 0, None)
            mixed = twice[0:cols] + twice[cols:]
            if inner:
                direction = dot(mix, stack[x - 1, y - 1], 1, 0)
                stack2[x - 1, y - 1, 0:cols, :] = direction
                mixed = jnp.concatenate([direction, mixed], axis=1)
            field[x, y] = mixed.astype(BF16).astype(F32)

    def write_second(x, y, image):
        stack2[x, y, cols:, :] = image

    operate(lambda x, y: stack2[x, y, 0:cols, :], write_second)
    sum_start(1, 0, pack(gram(stack2)))
    for x, y in own:
        sol_ref[x, y] = dot(alpha_t, stack[x, y, 0:cols, :], 1, 0)
        res_ref[x, y] = stack[x, y, 0:cols, :] - dot(alpha_t, stack[x, y, cols:, :], 1, 0)
    halo_left(0, padded, sides)
    halo_left(1, padded_im, sides_im)
    sum_left(0)
    table2 = sum_rest(1)
    curve2 = 0.5 * (table2[0:cols, cols:] + table2[cols:, 0:cols])
    alpha2_t = eliminate(curve2, updated).T
    for x, y in own:
        sol_ref[x, y] = sol_ref[x, y] + dot(alpha2_t, stack2[x, y, 0:cols, :], 1, 0)
        res_ref[x, y] = res_ref[x, y] - dot(alpha2_t, stack2[x, y, cols:, :], 1, 0)
    sum_left(1)


def on_device(sizes, loads, moduli, material):
    cols, nx, ny, nz = loads.shape
    count = int(np.prod(sizes))
    phases = (AXES,) if count <= DIRECT_LIMIT else (("gx", "gy"), ("gz",))
    slots = sum(int(np.prod([sizes[AXES.index(a)] for a in axes])) for axes in phases)
    body = functools.partial(kernel_body, sizes, phases, stiffness_values())
    out = jax.ShapeDtypeStruct((nx, ny, cols, nz), F32)
    vmem = pl.BlockSpec(memory_space=pltpu.VMEM)
    full = nz + LANES
    sol, res = pl.pallas_call(
        body,
        out_shape=(out, out),
        in_specs=[pl.BlockSpec(memory_space=pltpu.SMEM), vmem, vmem],
        out_specs=(vmem, vmem),
        scratch_shapes=[
            pltpu.VMEM((nx, ny, 2 * cols, nz), F32),
            pltpu.VMEM((nx + 2, ny + 2, 2 * cols, nz), BF16),
            pltpu.VMEM((2, nx + 2, ny + 2, 2 * cols, LANES), BF16),
            pltpu.VMEM((nx + 2, ny + 2, cols, nz), BF16),
            pltpu.VMEM((2, nx + 2, ny + 2, cols, LANES), BF16),
            pltpu.VMEM((nx + 2, ny + 2, cols, full), F32),
            pltpu.VMEM((nx + 1, ny + 1, 8, full), F32),
            pltpu.VMEM((nx + 1, ny + 1, 8, full), F32),
            pltpu.VMEM((nx, ny, 2 * cols, nz), F32),
            pltpu.VMEM((2, slots, 8, LANES), F32),
            pltpu.SemaphoreType.DMA((2, 26)),
            pltpu.SemaphoreType.DMA((2, 26)),
            pltpu.SemaphoreType.DMA((2, slots)),
            pltpu.SemaphoreType.DMA((2, slots)),
        ],
        compiler_params=pltpu.CompilerParams(collective_id=0, has_side_effects=True),
    )(moduli, loads.transpose(1, 2, 0, 3), material.reshape(nx * ny, nz))
    return sol.transpose(2, 0, 1, 3), res.transpose(2, 0, 1, 3)


def solution(mesh):
    sizes = tuple(mesh.shape[axis] for axis in AXES)
    in_specs = (P(None, "gx", "gy", "gz"), P(), P("gx", "gy", "gz"))
    out_specs = (P(None, "gx", "gy", "gz"), P(None, "gx", "gy", "gz"))
    return jax.shard_map(
        functools.partial(on_device, sizes), mesh=mesh, in_specs=in_specs, out_specs=out_specs, check_vma=False
    )
```

time: 187 us -> 40.9 us (0.22)
  blocking collectives: 82.4 us -> 0 us
  starting transfers between devices: 40 us -> 0 us
  Pallas kernels: 0 us -> 34.7 us
  waiting for transfers between devices: 26.4 us -> 0 us
  other arithmetic: 15.8 us -> 0 us
  matrix products: 13.6 us -> 0 us
    psum x2 -> x0, blocking collectives: 82.4 us -> none  [the longest x1 43.2 us: residual_gram(): return lax.psum(local_gram(residual, residual), ('gx', 'gy', 'gz'))]
    ppermute x18 -> x0, starting transfers between devices: 40 us -> none  [the longest x9 28.4 us: padded_2(): lax.ppermute(tail, axis, [(i, (i + 1) % count) for i in range(ends)])]
    pallas_call x0 -> x1, Pallas kernels: none -> 34.7 us  [on_device(): pl.pallas_call(body, out_shape=(out, out), in_specs=[pl.BlockSpec(memory_...]
    ppermute x18 -> x0, waiting for transfers between devices: 26.4 us -> none  [the longest x9 24.2 us: padded_2(): lax.ppermute(head, axis, [((i + 1) % count, i) for i in range(ends)])]
    dot_general x28 -> x0, matrix products: 12.5 us -> none  [the longest x16 8.36 us: apply_operator(): jnp.einsum('b,bcxyz->cxyz', kernel[corner], stacked, preferred_element_ty...]
    another operation x15 -> x0, other arithmetic: 12 us -> none  [the longest x9 6.4 us: solve_small(): factor = jnp.linalg.cholesky(matrix)]
    unnamed x34 -> x5, local copies, waits for them, and re-layouts: 3.07 us -> 4.03 us
  transfers between devices with their start and end apart: 18 -> 0, of which waited for: 12 -> 0; matrix products, arithmetic and copies ran while one was open for 2% -> 0% of each run, Pallas kernels for 0% -> 0%
where the time goes in v1:
time: 40.9 us; the launch traced here: 40.6 us
  Pallas kernels  34.7 us (85%)
  local copies, waits for them, and re-layouts  5.33 us (13%)
  between operations  0.65 us (2%)
    pallas_call x1, Pallas kernels, on_device(): pl.pallas_call(body, out_shape=(out, out), in_specs=[pl.BlockSpec(memory_...  34.7 us
    unnamed x5, local copies, waits for them, and re-layouts  4.03 us
    reshape x1, local copies, waits for them, and re-layouts, on_device(): material.reshape(nx * ny, nz)  1.3 us

profile of v1, /device:TPU:0, one launch (start us, length us, event | category | flops | bytes accessed | tf_op | source)
XLA Modules:
  0.0 40.6 jit_solution(16651143272008816960)
XLA Ops:
  0.6 1.3 %reshape.7.mat_ref = s32[8,256]{1,0:T(8,128)} reshape(s32[2,4,256]{2,1,0:T(4,128)} %param.5) | data formatting | bytes 16384 | tf_op jit(solution)/shard_map/reshape | solution.py:411
  1.9 1.6 %copy.9 = f32[16,2,4,256]{3,0,2,1:T(8,128)} copy(f32[16,2,4,256]{3,2,1,0:T(4,128)} %param.3) | data formatting | bytes 262144 | tf_op args[0]
  3.5 34.7 %shard_map.50 = (f32[2,4,16,256]{3,2,1,0:T(8,128)}, f32[2,4,16,256]{3,2,1,0:T(8,128)}) custom-call(f32[8]{0:T(128)} %moduli_ref.1, f32[2,4,16,256]{3,2,1,0:T(8,128)} %bitcast.5, s32[8,256]{1,0:T(8,128)} %reshape.7.mat_ref), custom_call_target="tpu_custom_call" | custom-call | tf_op jit(solution)/shard_map/pallas_call | solution.py:389
  38.2 0.0 copy-start
  38.2 1.7 %copy.6 = f32[16,2,4,256]{3,2,1,0:T(4,128)} copy(f32[16,2,4,256]{3,0,2,1:T(8,128)} %bitcast.7) | data formatting | bytes 262144
  39.9 0.0 copy-done
  39.9 0.7 %copy.7 = f32[16,2,4,256]{3,2,1,0:T(4,128)} copy(f32[16,2,4,256]{3,0,2,1:T(8,128)S(1)} %bitcast.6) | data formatting | bytes 262144
Async XLA Ops:
  38.2 1.7 %copy-start = (f32[2,4,16,256]{3,2,1,0:T(8,128)S(1)}, f32[2,4,16,256]{3,2,1,0:T(8,128)}, u32[]{:S(2)}) copy-start(f32[2,4,16,256]{3,2,1,0:T(8,128)} %get-tuple-element.5) | copy-start | bytes 393220

commit v2 on v1

--- a/solution.py
+++ b/solution.py
@@ -68,9 +68,9 @@
 
 def kernel_body(sizes, phases, stiff, moduli_ref, loads_ref, mat_ref, sol_ref, res_ref,
                 stack, padded, sides, padded_im, sides_im, field, wt, wtr, stack2, shares,
-                halo_send, halo_recv, sum_send, sum_recv):
-    cols = loads_ref.shape[2]
-    nx, ny, nz = loads_ref.shape[0], loads_ref.shape[1], loads_ref.shape[3]
+                halo_send, halo_recv, sum_send, sum_recv,
+                out_stage, local_sems):
+    cols, nx, ny, nz = loads_ref.shape
     mats = moduli_ref.shape[0]
     me = [lax.axis_index(axis) for axis in AXES]
     k_self, k_edge, k_far = stiff[0], stiff[1], stiff[2]
@@ -151,6 +151,19 @@
         offsets.append(total_slots)
         total_slots += group_of(axes)[0]
 
+    def fetch(x, y):
+        return pltpu.make_async_copy(
+            loads_ref.at[:, x, y, :], stack.at[x, y, pl.ds(0, cols), :], local_sems.at[0, x * ny + y]
+        )
+
+    def put(which, ref, x, y):
+        return pltpu.make_async_copy(
+            out_stage.at[which, x, y], ref.at[:, x, y, :], local_sems.at[1 + which, x * ny + y]
+        )
+
+    for x, y in own:
+        fetch(x, y).start()
+
     for x in xs:
         for y in ys:
             padded[x, y] = jnp.zeros(padded.shape[2:], BF16)
@@ -182,11 +195,10 @@
             expected = expected + jnp.where(good, 1, 0)
 
     for x, y in own:
-        values = loads_ref[x, y]
-        stack[x, y, 0:cols, :] = values
+        fetch(x, y).wait()
+        values = stack[x, y, 0:cols, :]
         padded[x + 1, y + 1, 0:cols, :] = values.astype(BF16)
-        row = x * ny + y
-        ids = (mat_ref[row : row + 1, :] + 1).astype(F32)
+        ids = (mat_ref[x, y : y + 1, :] + 1).astype(F32)
         padded[x + 1, y + 1, cols:, :] = jnp.broadcast_to(ids, (cols, nz)).astype(BF16)
     pl.semaphore_wait(barrier, expected)
     halo_start(0, padded, sides)
@@ -363,8 +375,8 @@
     operate(lambda x, y: stack2[x, y, 0:cols, :], write_second)
     sum_start(1, 0, pack(gram(stack2)))
     for x, y in own:
-        sol_ref[x, y] = dot(alpha_t, stack[x, y, 0:cols, :], 1, 0)
-        res_ref[x, y] = stack[x, y, 0:cols, :] - dot(alpha_t, stack[x, y, cols:, :], 1, 0)
+        out_stage[0, x, y] = dot(alpha_t, stack[x, y, 0:cols, :], 1, 0)
+        out_stage[1, x, y] = stack[x, y, 0:cols, :] - dot(alpha_t, stack[x, y, cols:, :], 1, 0)
     halo_left(0, padded, sides)
     halo_left(1, padded_im, sides_im)
     sum_left(0)
@@ -372,9 +384,14 @@
     curve2 = 0.5 * (table2[0:cols, cols:] + table2[cols:, 0:cols])
     alpha2_t = eliminate(curve2, updated).T
     for x, y in own:
-        sol_ref[x, y] = sol_ref[x, y] + dot(alpha2_t, stack2[x, y, 0:cols, :], 1, 0)
-        res_ref[x, y] = res_ref[x, y] - dot(alpha2_t, stack2[x, y, cols:, :], 1, 0)
+        out_stage[0, x, y] = out_stage[0, x, y] + dot(alpha2_t, stack2[x, y, 0:cols, :], 1, 0)
+        put(0, sol_ref, x, y).start()
+        out_stage[1, x, y] = out_stage[1, x, y] - dot(alpha2_t, stack2[x, y, cols:, :], 1, 0)
+        put(1, res_ref, x, y).start()
     sum_left(1)
+    for x, y in own:
+        put(0, sol_ref, x, y).wait()
+        put(1, res_ref, x, y).wait()
 
 
 def on_device(sizes, loads, moduli, material):
@@ -383,14 +400,15 @@
     phases = (AXES,) if count <= DIRECT_LIMIT else (("gx", "gy"), ("gz",))
     slots = sum(int(np.prod([sizes[AXES.index(a)] for a in axes])) for axes in phases)
     body = functools.partial(kernel_body, sizes, phases, stiffness_values())
-    out = jax.ShapeDtypeStruct((nx, ny, cols, nz), F32)
+    out = jax.ShapeDtypeStruct((cols, nx, ny, nz), F32)
     vmem = pl.BlockSpec(memory_space=pltpu.VMEM)
+    anywhere = pl.BlockSpec(memory_space=pl.ANY)
     full = nz + LANES
-    sol, res = pl.pallas_call(
+    return pl.pallas_call(
         body,
         out_shape=(out, out),
-        in_specs=[pl.BlockSpec(memory_space=pltpu.SMEM), vmem, vmem],
-        out_specs=(vmem, vmem),
+        in_specs=[pl.BlockSpec(memory_space=pltpu.SMEM), anywhere, vmem],
+        out_specs=(anywhere, anywhere),
         scratch_shapes=[
             pltpu.VMEM((nx, ny, 2 * cols, nz), F32),
             pltpu.VMEM((nx + 2, ny + 2, 2 * cols, nz), BF16),
@@ -406,10 +424,11 @@
             pltpu.SemaphoreType.DMA((2, 26)),
             pltpu.SemaphoreType.DMA((2, slots)),
             pltpu.SemaphoreType.DMA((2, slots)),
+            pltpu.VMEM((2, nx, ny, cols, nz), F32),
+            pltpu.SemaphoreType.DMA((3, nx * ny)),
         ],
         compiler_params=pltpu.CompilerParams(collective_id=0, has_side_effects=True),
-    )(moduli, loads.transpose(1, 2, 0, 3), material.reshape(nx * ny, nz))
-    return sol.transpose(2, 0, 1, 3), res.transpose(2, 0, 1, 3)
+    )(moduli, loads, material)
 
 
 def solution(mesh):

time: 40.9 us -> 39.7 us (0.971)
  local copies, waits for them, and re-layouts: 5.33 us -> 2.26 us
  Pallas kernels: 34.7 us -> 36.6 us
    pallas_call x1, Pallas kernels: 34.7 us -> 36.6 us  [on_device(): pl.pallas_call(body, out_shape=(out, out), in_specs=[pl.BlockSpec(memory_...]
    unnamed x5 -> x4, local copies, waits for them, and re-layouts: 4.03 us -> 2.26 us
    reshape x1 -> x0, local copies, waits for them, and re-layouts: 1.3 us -> none  [on_device(): material.reshape(nx * ny, nz)]
where the time goes in v2:
time: 39.7 us; the launch traced here: 39.5 us
  Pallas kernels  36.6 us (92%)
  local copies, waits for them, and re-layouts  2.26 us (6%)
  between operations  0.65 us (2%)
    pallas_call x1, Pallas kernels, on_device(): pl.pallas_call(body, out_shape=(out, out), in_specs=[pl.BlockSpec(memory_...  36.6 us
    unnamed x4, local copies, waits for them, and re-layouts  2.26 us

profile of v2, /device:TPU:0, one launch (start us, length us, event | category | flops | bytes accessed | tf_op | source)
XLA Modules:
  0.0 39.5 jit_solution(2277554643362047037)
XLA Ops:
  0.6 36.6 %shard_map.50 = (f32[16,2,4,256]{3,2,1,0:T(4,128)}, f32[16,2,4,256]{3,2,1,0:T(4,128)}) custom-call(f32[8]{0:T(128)} %moduli_ref.1, f32[16,2,4,256]{3,2,1,0:T(4,128)} %loads_ref.1, s32[2,4,256]{2,1,0:T(4,128)} %mat_ref.1), custom_call_target="tpu_custom_call" | custom-call | tf_op jit(solution)/shard_map/pallas_call | solution.py:407
  37.2 0.0 copy-start
  37.3 1.6 %copy.7 = f32[16,2,4,256]{3,2,1,0:T(4,128)} copy(f32[16,2,4,256]{3,2,1,0:T(4,128)} %get-tuple-element.4) | data formatting | bytes 262144
  38.9 0.0 copy-done
  38.9 0.7 %copy.8 = f32[16,2,4,256]{3,2,1,0:T(4,128)} copy(f32[16,2,4,256]{3,2,1,0:T(4,128)S(1)} %copy-done) | data formatting | bytes 262144
Async XLA Ops:
  37.2 1.6 %copy-start = (f32[16,2,4,256]{3,2,1,0:T(4,128)S(1)}, f32[16,2,4,256]{3,2,1,0:T(4,128)}, u32[]{:S(2)}) copy-start(f32[16,2,4,256]{3,2,1,0:T(4,128)} %get-tuple-element.5) | copy-start | bytes 393220

commit v3 on v2

v3 whole, which is shorter than its diff:
```python
import functools
import itertools

import jax
import jax.numpy as jnp
import numpy as np
from jax import lax
from jax.experimental import pallas as pl
from jax.experimental.pallas import tpu as pltpu
from jax.sharding import PartitionSpec as P

SIGMA = 0.25
AXES = ("gx", "gy", "gz")
HIGH = lax.Precision.HIGHEST
F32 = jnp.float32
BF16 = jnp.bfloat16
LANES = 128
DIRECT_LIMIT = 32


def stiffness_values():
    mass = (1.0 / 3.0, 1.0 / 6.0)
    stiff = (1.0, -1.0)
    values = []
    for differing in range(4):
        bits = [1 if dim < differing else 0 for dim in range(3)]
        total = 0.0
        for dim in range(3):
            factor = 1.0
            for other in range(3):
                factor *= stiff[bits[other]] if other == dim else mass[bits[other]]
            total += factor
        values.append(float(np.asarray(total, np.float32).astype(jnp.bfloat16).astype(np.float32)))
    return values


def dot(left, right, left_dim, right_dim, precision=HIGH):
    return lax.dot_general(
        left, right, (((left_dim,), (right_dim,)), ((), ())), precision=precision, preferred_element_type=F32
    )


def pack(matrix):
    rows, cols = matrix.shape
    wide = jnp.concatenate([matrix, jnp.zeros((rows, LANES - cols), F32)], axis=1)
    pieces = [
        jnp.sum(pltpu.roll(wide[start : start + 8], 0, 1, stride=cols, stride_axis=0), axis=0, keepdims=True)
        for start in range(0, rows, 8)
    ]
    return jnp.concatenate(pieces, axis=0)


def unpack(tile, cols):
    rows = tile.shape[0]
    tall = jnp.concatenate([tile, jnp.zeros((8 - rows, LANES), F32)], axis=0)
    turned = [tall] + [pltpu.roll(tall, LANES - cols * group, 1) for group in range(1, 8)]
    return jnp.concatenate(
        [turned[group][row : row + 1] for row in range(rows) for group in range(8)], axis=0
    )[:, 0:cols]


def eliminate(matrix, rhs):
    size = matrix.shape[0]
    both = jnp.concatenate([matrix, rhs], axis=1)
    rows = lax.broadcasted_iota(jnp.int32, both.shape, 0)
    for step in range(0, size, 2):
        top, low = both[step : step + 1, :], both[step + 1 : step + 2, :]
        left, right = both[:, step : step + 1], both[:, step + 1 : step + 2]
        first, mixed, second = top[:, step : step + 1], top[:, step + 1 : step + 2], low[:, step + 1 : step + 2]
        ratio = mixed / first
        low_new = (low - ratio * top) / (second - ratio * mixed)
        top_new = top / first - ratio * low_new
        rest = both - left * top_new - right * low_new
        both = jnp.where(rows == step, top_new, jnp.where(rows == step + 1, low_new, rest))
    return both[:, size:]


def kernel_body(sizes, phases, stiff, moduli_ref, loads_ref, mat_ref, sol_ref, res_ref,
                stack, padded, padded_im, mats_rx, ends, ends_rx, ends_im, ends_im_rx, field, wt, wtr, stack2,
                shares_rr, shares_im, shares_last, halo_send, halo_recv, sum_send, sum_recv,
                out_stage, local_sems):
    cols, nx, ny, nz = loads_ref.shape
    mats = moduli_ref.shape[0]
    me = [lax.axis_index(axis) for axis in AXES]
    k_self, k_edge, k_far = stiff[0], stiff[1], stiff[2]
    assert k_edge == 0.0 and stiff[2] == stiff[3]
    xs, ys = range(nx + 2), range(ny + 2)
    shares_of = (shares_rr, shares_im, shares_last)
    own = list(itertools.product(range(nx), range(ny)))

    directions = [
        d for d in itertools.product((-1, 0, 1), repeat=3)
        if any(d) and all(step == 0 or sizes[i] > 1 for i, step in enumerate(d))
    ]

    def exists(direction):
        good = None
        for i, step in enumerate(direction):
            if step:
                here = (me[i] > 0) if step < 0 else (me[i] < sizes[i] - 1)
                good = here if good is None else jnp.logical_and(good, here)
        return good

    def target(direction):
        return {axis: me[i] + direction[i] for i, axis in enumerate(AXES)}

    def place(direction):
        return 1 - direction[0], 1 - direction[1]

    def halo_copies(round_, number):
        direction = dx, dy, dz = directions[number]
        core, source, edge = ((padded, ends, ends_rx), (padded_im, ends_im, ends_im_rx))[round_]
        pairs = []
        if dz == 0:
            src_x = {0: pl.ds(1, nx), 1: pl.ds(nx, 1), -1: pl.ds(1, 1)}[dx]
            dst_x = {0: pl.ds(1, nx), 1: pl.ds(0, 1), -1: pl.ds(nx + 1, 1)}[dx]
            src_y = {0: pl.ds(1, ny), 1: pl.ds(ny, 1), -1: pl.ds(1, 1)}[dy]
            dst_y = {0: pl.ds(1, ny), 1: pl.ds(0, 1), -1: pl.ds(ny + 1, 1)}[dy]
            pairs.append((core.at[src_x, src_y], core.at[dst_x, dst_y]))
            if round_ == 0:
                pairs.append((mats_rx.at[1, 1], mats_rx.at[place(direction)]))
        else:
            pairs.append((source.at[1 if dz > 0 else 0], edge.at[(*place(direction), 0 if dz > 0 else 1)]))
        return [
            pltpu.make_async_remote_copy(
                src_ref=src, dst_ref=dst, send_sem=halo_send.at[round_ + 2 * i, number],
                recv_sem=halo_recv.at[round_ + 2 * i, number],
                device_id=target(direction), device_id_type=pl.DeviceIdType.MESH,
            )
            for i, (src, dst) in enumerate(pairs)
        ]

    def halo_each(round_, act, incoming=False):
        for number, direction in enumerate(directions):
            @pl.when(exists(tuple(-step for step in direction) if incoming else direction))
            def _():
                for copy in halo_copies(round_, number):
                    act(copy)

    def halo_start(round_):
        halo_each(round_, lambda copy: copy.start())

    def halo_arrive(round_):
        halo_each(round_, lambda copy: copy.wait_recv(), True)

    def halo_left(round_):
        halo_each(round_, lambda copy: copy.wait_send())

    def each(count, body):
        if count <= 8:
            for k in range(1, count):
                body(k, 0)
        else:
            lax.fori_loop(1, count, body, 0)

    def group_of(axes):
        count, index = 1, 0
        for axis in axes:
            i = AXES.index(axis)
            count *= sizes[i]
            index = index * sizes[i] + me[i]
        return count, index

    def peer_id(axes, peer):
        coords = {axis: me[i] for i, axis in enumerate(AXES)}
        for axis in reversed(axes):
            size = sizes[AXES.index(axis)]
            coords[axis] = lax.rem(peer, size)
            peer = lax.div(peer, size)
        return coords

    offsets = []
    total_slots = 0
    for axes in phases:
        offsets.append(total_slots)
        total_slots += group_of(axes)[0]

    def fetch(x, y):
        return pltpu.make_async_copy(
            loads_ref.at[:, x, y, :], stack.at[x, y, pl.ds(0, cols), :], local_sems.at[0, x * ny + y]
        )

    def put(which, ref, x, y):
        return pltpu.make_async_copy(
            out_stage.at[which, x, y], ref.at[:, x, y, :], local_sems.at[1 + which, x * ny + y]
        )

    for x, y in own:
        fetch(x, y).start()

    for x in xs:
        for y in ys:
            if not (1 <= x <= nx and 1 <= y <= ny):
                padded[x, y] = jnp.zeros(padded.shape[2:], BF16)
                padded_im[x, y] = jnp.zeros(padded_im.shape[2:], BF16)
    for bx, by in itertools.product(range(3), repeat=2):
        mats_rx[bx, by] = jnp.zeros(mats_rx.shape[2:], F32)
        for side in range(2):
            ends_rx[bx, by, side] = jnp.zeros(ends_rx.shape[3:], BF16)
            ends_im_rx[bx, by, side] = jnp.zeros(ends_im_rx.shape[3:], BF16)

    barrier = pltpu.get_barrier_semaphore()
    expected = 0
    for axes in phases:
        count, index = group_of(axes)

        def greet(k, carry, axes=axes, count=count, index=index):
            pl.semaphore_signal(barrier, inc=1, device_id=peer_id(axes, lax.rem(index + k, count)),
                                device_id_type=pl.DeviceIdType.MESH)
            return carry

        each(count, greet)
        expected = expected + count - 1
    if len(phases) > 1:
        for direction in directions:
            good = exists(direction)

            @pl.when(good)
            def _():
                pl.semaphore_signal(barrier, inc=1, device_id=target(direction),
                                    device_id_type=pl.DeviceIdType.MESH)
            expected = expected + jnp.where(good, 1, 0)

    lane = lax.broadcasted_iota(jnp.int32, (1, LANES), 1)
    firsts = lasts = jnp.zeros((2 * cols, LANES), F32)
    for x in range(nx):
        mats_rx[1, 1, x * ny : (x + 1) * ny, :] = (mat_ref[x] + 1).astype(F32)
    for x, y in own:
        fetch(x, y).wait()
        values = stack[x, y, 0:cols, :]
        padded[x + 1, y + 1] = values.astype(BF16)
        row = x * ny + y
        ids = jnp.broadcast_to(mats_rx[1, 1, row : row + 1, :], (cols, nz))
        column = jnp.concatenate([values, ids], axis=0)
        firsts = jnp.where(lane == row, column[:, 0:1], firsts)
        lasts = jnp.where(lane == row, column[:, nz - 1 : nz], lasts)
    ends[0] = firsts.astype(BF16)
    ends[1] = lasts.astype(BF16)
    pl.semaphore_wait(barrier, expected)
    halo_start(0)

    def block_of(x, y):
        bx, lx = (0, nx - 1) if x == 0 else (2, 0) if x == nx + 1 else (1, x - 1)
        by, ly = (0, ny - 1) if y == 0 else (2, 0) if y == ny + 1 else (1, y - 1)
        return bx, by, lx * ny + ly

    def merged(edge, x, y):
        bx, by, row = block_of(x, y)
        left, right = edge[bx, by, 0].astype(F32), edge[bx, by, 1].astype(F32)
        return jnp.where(lane == 0, right[:, row : row + 1],
                         jnp.where(lane == LANES - 1, left[:, row : row + 1], 0.0))

    def gram(left, right):
        total = None
        for x, y in own:
            part = dot(left(x, y), right(x, y), 1, 1)
            total = part if total is None else total + part
        return total

    def sum_copy(round_, number, k):
        axes = phases[number]
        count, index = group_of(axes)
        slot = offsets[number] + index
        return pltpu.make_async_remote_copy(
            src_ref=shares_of[round_].at[slot], dst_ref=shares_of[round_].at[slot],
            send_sem=sum_send.at[round_, offsets[number] + k], recv_sem=sum_recv.at[round_, offsets[number] + k],
            device_id=peer_id(axes, lax.rem(index + k, count)), device_id_type=pl.DeviceIdType.MESH,
        )

    def sum_arrival(round_, number, k):
        axes = phases[number]
        count, index = group_of(axes)
        source = lax.rem(index + count - k, count)
        slot = offsets[number] + source
        return pltpu.make_async_remote_copy(
            src_ref=shares_of[round_].at[slot], dst_ref=shares_of[round_].at[slot],
            send_sem=sum_send.at[round_, offsets[number] + k], recv_sem=sum_recv.at[round_, offsets[number] + k],
            device_id=peer_id(axes, lax.rem(index + k, count)), device_id_type=pl.DeviceIdType.MESH,
        )

    def sum_start(round_, number, tile):
        count, index = group_of(phases[number])
        shares_of[round_][offsets[number] + index] = tile

        def send(k, carry):
            sum_copy(round_, number, k).start()
            return carry

        each(count, send)

    def sum_finish(round_, number):
        count, _ = group_of(phases[number])

        def receive(k, carry):
            sum_arrival(round_, number, k).wait_recv()
            return carry

        each(count, receive)
        tile = shares_of[round_][offsets[number]]
        for peer in range(1, count):
            tile = tile + shares_of[round_][offsets[number] + peer]
        return tile

    def sum_turn(round_):
        for number in range(1, len(phases)):
            sum_start(round_, number, sum_finish(round_, number - 1))

    def sum_rest(round_):
        return unpack(sum_finish(round_, len(phases) - 1), cols)

    def sum_left(round_):
        for number, axes in enumerate(phases):
            def drain(k, carry, number=number):
                sum_copy(round_, number, k).wait_send()
                return carry

            each(group_of(axes)[0], drain)

    def loads_at(x, y):
        return stack[x, y, 0:cols, :]

    def image_at(x, y):
        return stack[x, y, cols:, :]

    def loads_at2(x, y):
        return stack2[x, y, 0:cols, :]

    def image_at2(x, y):
        return stack2[x, y, cols:, :]

    sum_start(0, 0, pack(gram(loads_at, loads_at)))
    halo_arrive(0)
    sum_turn(0)
    full = nz + LANES
    moduli = {}
    for x in xs:
        for y in ys:
            tail = merged(ends_rx, x, y)
            field[x, y] = jnp.concatenate([padded[x, y].astype(F32), tail[0:cols]], axis=1)
            bx, by, row = block_of(x, y)
            ids = jnp.concatenate([
                jnp.broadcast_to(mats_rx[bx, by, row : row + 1, :], (8, nz)), tail[cols : cols + 8]
            ], axis=1)
            modulus = jnp.zeros_like(ids)
            for number in range(mats):
                modulus = modulus + jnp.where(ids == float(number + 1), moduli_ref[number], 0.0)
            moduli[x, y] = modulus
    for x in range(nx + 1):
        for y in range(ny + 1):
            total = (moduli[x, y] + moduli[x, y + 1]) + (moduli[x + 1, y] + moduli[x + 1, y + 1])
            weight = 0.125 * (total + pltpu.roll(total, full - 1, 1))
            wt[x, y] = weight
            wtr[x, y] = pltpu.roll(weight, 1, 1)

    def double(tile):
        return jnp.concatenate([tile, tile], axis=0)

    def operate(direction_of, write):
        for x in range(nx):
            for y in range(ny):
                here = field[x + 1, y + 1]
                ahead = behind = flat = None
                w_ahead = w_behind = None
                for ex in (x, x + 1):
                    for ey in (y, y + 1):
                        corner_sum = (field[ex, ey] + field[ex, ey + 1]) + (field[ex + 1, ey] + field[ex + 1, ey + 1])
                        after, before = wt[ex, ey], wtr[ex, ey]
                        opposite = field[2 * ex - x, 2 * ey - y][:, 0:nz]
                        one = double(before) * corner_sum
                        two = double(after) * corner_sum
                        three = double((before + after)[:, 0:nz]) * opposite
                        ahead = one if ahead is None else ahead + one
                        behind = two if behind is None else behind + two
                        flat = three if flat is None else flat + three
                        w_ahead = before if w_ahead is None else w_ahead + before
                        w_behind = after if w_behind is None else w_behind + after
                ahead = ahead - double(w_ahead) * here
                behind = behind - double(w_behind) * here
                around = pltpu.roll(ahead, full - 1, 1)[:, 0:nz] + pltpu.roll(behind, 1, 1)[:, 0:nz] + flat
                centre = double((w_ahead + w_behind)[:, 0:nz]) * here[:, 0:nz]
                write(x, y, SIGMA * direction_of(x, y) + (k_far * around + k_self * centre))

    image_firsts = jnp.zeros((cols, LANES), F32)
    image_ends = [image_firsts, image_firsts]

    def write_first(x, y, image):
        stack[x, y, cols:, :] = image
        padded_im[x + 1, y + 1] = image.astype(BF16)
        row = x * ny + y
        image_ends[0] = jnp.where(lane == row, image[:, 0:1], image_ends[0])
        image_ends[1] = jnp.where(lane == row, image[:, nz - 1 : nz], image_ends[1])

    operate(loads_at, write_first)
    ends_im[0] = image_ends[0].astype(BF16)
    ends_im[1] = image_ends[1].astype(BF16)
    cross_part = gram(image_at, lambda x, y: stack[x, y])
    sum_start(1, 0, jnp.concatenate([pack(cross_part[:, 0:cols]), pack(cross_part[:, cols:])], axis=0))
    halo_start(1)
    square = sum_rest(0)
    sum_turn(1)
    row_id = lax.broadcasted_iota(jnp.int32, (cols, cols), 0)
    col_id = lax.broadcasted_iota(jnp.int32, (cols, cols), 1)
    eye = jnp.where(row_id == col_id, 1.0, 0.0)
    inverse = eliminate(square, eye)
    table = sum_rest(1)

    cross, quad = table[0:cols], table[cols:]
    alpha = eliminate(0.5 * (cross + cross.T), square)
    updated = square + dot(alpha, dot(quad, alpha, 1, 0) - cross, 0, 0) - dot(cross, alpha, 0, 0)
    beta = dot(inverse, updated, 1, 0)
    alpha_t = alpha.T
    mix = jnp.concatenate([(eye + beta).T, -alpha_t], axis=1)
    mix_hi = mix.astype(BF16)
    mix_lo = (mix - mix_hi.astype(F32)).astype(BF16)
    mix_both = jnp.concatenate([mix_hi, mix_lo], axis=0)

    halo_arrive(1)
    for x in xs:
        for y in ys:
            inner = 1 <= x <= nx and 1 <= y <= ny
            tail_l = merged(ends_rx, x, y)[0:cols].astype(BF16)
            tail_i = merged(ends_im_rx, x, y).astype(BF16)
            if inner:
                near = jnp.concatenate([tail_l, tail_i], axis=0)
            else:
                near = jnp.concatenate([
                    jnp.concatenate([padded[x, y], tail_l], axis=1),
                    jnp.concatenate([padded_im[x, y], tail_i], axis=1),
                ], axis=0)
            twice = dot(mix_both, near, 1, 0, None)
            mixed = twice[0:cols] + twice[cols:]
            if inner:
                direction = dot(mix, stack[x - 1, y - 1], 1, 0)
                stack2[x - 1, y - 1, 0:cols, :] = direction
                mixed = jnp.concatenate([direction, mixed], axis=1)
            field[x, y] = mixed.astype(BF16).astype(F32)

    def write_second(x, y, image):
        stack2[x, y, cols:, :] = image

    operate(loads_at2, write_second)
    sum_start(2, 0, pack(gram(image_at2, loads_at2)))
    for x, y in own:
        out_stage[0, x, y] = dot(alpha_t, stack[x, y, 0:cols, :], 1, 0)
        out_stage[1, x, y] = stack[x, y, 0:cols, :] - dot(alpha_t, stack[x, y, cols:, :], 1, 0)
    halo_left(0)
    halo_left(1)
    sum_left(0)
    sum_left(1)
    sum_turn(2)
    cross2 = sum_rest(2)
    alpha2_t = eliminate(0.5 * (cross2 + cross2.T), updated).T
    for x, y in own:
        out_stage[0, x, y] = out_stage[0, x, y] + dot(alpha2_t, stack2[x, y, 0:cols, :], 1, 0)
        put(0, sol_ref, x, y).start()
        out_stage[1, x, y] = out_stage[1, x, y] - dot(alpha2_t, stack2[x, y, cols:, :], 1, 0)
        put(1, res_ref, x, y).start()
    sum_left(2)
    for x, y in own:
        put(0, sol_ref, x, y).wait()
        put(1, res_ref, x, y).wait()


def on_device(sizes, loads, moduli, material):
    cols, nx, ny, nz = loads.shape
    count = int(np.prod(sizes))
    phases = (AXES,) if count <= DIRECT_LIMIT else (("gx", "gy"), ("gz",))
    slots = sum(int(np.prod([sizes[AXES.index(a)] for a in axes])) for axes in phases)
    body = functools.partial(kernel_body, sizes, phases, stiffness_values())
    out = jax.ShapeDtypeStruct((cols, nx, ny, nz), F32)
    vmem = pl.BlockSpec(memory_space=pltpu.VMEM)
    anywhere = pl.BlockSpec(memory_space=pl.ANY)
    full = nz + LANES
    return pl.pallas_call(
        body,
        out_shape=(out, out),
        in_specs=[pl.BlockSpec(memory_space=pltpu.SMEM), anywhere, vmem],
        out_specs=(anywhere, anywhere),
        scratch_shapes=[
            pltpu.VMEM((nx, ny, 2 * cols, nz), F32),
            pltpu.VMEM((nx + 2, ny + 2, cols, nz), BF16),
            pltpu.VMEM((nx + 2, ny + 2, cols, nz), BF16),
            pltpu.VMEM((3, 3, nx * ny, nz), F32),
            pltpu.VMEM((2, 2 * cols, LANES), BF16),
            pltpu.VMEM((3, 3, 2, 2 * cols, LANES), BF16),
            pltpu.VMEM((2, cols, LANES), BF16),
            pltpu.VMEM((3, 3, 2, cols, LANES), BF16),
            pltpu.VMEM((nx + 2, ny + 2, cols, full), F32),
            pltpu.VMEM((nx + 1, ny + 1, 8, full), F32),
            pltpu.VMEM((nx + 1, ny + 1, 8, full), F32),
            pltpu.VMEM((nx, ny, 2 * cols, nz), F32),
            pltpu.VMEM((slots, cols * cols // LANES, LANES), F32),
            pltpu.VMEM((slots, 2 * cols * cols // LANES, LANES), F32),
            pltpu.VMEM((slots, cols * cols // LANES, LANES), F32),
            pltpu.SemaphoreType.DMA((3, 26)),
            pltpu.SemaphoreType.DMA((3, 26)),
            pltpu.SemaphoreType.DMA((3, slots)),
            pltpu.SemaphoreType.DMA((3, slots)),
            pltpu.VMEM((2, nx, ny, cols, nz), F32),
            pltpu.SemaphoreType.DMA((3, nx * ny)),
        ],
        compiler_params=pltpu.CompilerParams(collective_id=0, has_side_effects=True),
    )(moduli, loads, material)


def solution(mesh):
    sizes = tuple(mesh.shape[axis] for axis in AXES)
    in_specs = (P(None, "gx", "gy", "gz"), P(), P("gx", "gy", "gz"))
    out_specs = (P(None, "gx", "gy", "gz"), P(None, "gx", "gy", "gz"))
    return jax.shard_map(
        functools.partial(on_device, sizes), mesh=mesh, in_specs=in_specs, out_specs=out_specs, check_vma=False
    )
```

time: 39.7 us -> 37.6 us (0.947)
  Pallas kernels: 36.6 us -> 34.5 us
    pallas_call x1, Pallas kernels: 36.6 us -> 34.5 us  [on_device(): pl.pallas_call(body, out_shape=(out, out), in_specs=[pl.BlockSpec(memory_...]
where the time goes in v3:
time: 37.6 us; the launch traced here: 37.4 us
  Pallas kernels  34.5 us (92%)
  local copies, waits for them, and re-layouts  2.26 us (6%)
  between operations  0.65 us (2%)
    pallas_call x1, Pallas kernels, on_device(): pl.pallas_call(body, out_shape=(out, out), in_specs=[pl.BlockSpec(memory_...  34.5 us
    unnamed x4, local copies, waits for them, and re-layouts  2.26 us

profile of v3, /device:TPU:0, one launch (start us, length us, event | category | flops | bytes accessed | tf_op | source)
XLA Modules:
  0.0 37.4 jit_solution(15362138873713402391)
XLA Ops:
  0.6 34.5 %shard_map.50 = (f32[16,2,4,256]{3,2,1,0:T(4,128)}, f32[16,2,4,256]{3,2,1,0:T(4,128)}) custom-call(f32[8]{0:T(128)} %moduli_ref.1, f32[16,2,4,256]{3,2,1,0:T(4,128)} %loads_ref.1, s32[2,4,256]{2,1,0:T(4,128)} %mat_ref.1), custom_call_target="tpu_custom_call" | custom-call | tf_op jit(solution)/shard_map/pallas_call | solution.py:474
  35.1 0.0 copy-start
  35.1 1.6 %copy.7 = f32[16,2,4,256]{3,2,1,0:T(4,128)} copy(f32[16,2,4,256]{3,2,1,0:T(4,128)} %get-tuple-element.4) | data formatting | bytes 262144
  36.8 0.0 copy-done
  36.8 0.7 %copy.8 = f32[16,2,4,256]{3,2,1,0:T(4,128)} copy(f32[16,2,4,256]{3,2,1,0:T(4,128)S(1)} %copy-done) | data formatting | bytes 262144
Async XLA Ops:
  35.1 1.6 %copy-start = (f32[16,2,4,256]{3,2,1,0:T(4,128)S(1)}, f32[16,2,4,256]{3,2,1,0:T(4,128)}, u32[]{:S(2)}) copy-start(f32[16,2,4,256]{3,2,1,0:T(4,128)} %get-tuple-element.5) | copy-start | bytes 393220

commit v4 on v3

--- a/solution.py
+++ b/solution.py
@@ -78,7 +78,7 @@
 def kernel_body(sizes, phases, stiff, moduli_ref, loads_ref, mat_ref, sol_ref, res_ref,
                 stack, padded, padded_im, mats_rx, ends, ends_rx, ends_im, ends_im_rx, field, wt, wtr, stack2,
                 shares_rr, shares_im, shares_last, halo_send, halo_recv, sum_send, sum_recv,
-                out_stage, local_sems):
+                out_stage, local_sems, vouch_sem):
     cols, nx, ny, nz = loads_ref.shape
     mats = moduli_ref.shape[0]
     me = [lax.axis_index(axis) for axis in AXES]
@@ -201,17 +201,40 @@
 
     barrier = pltpu.get_barrier_semaphore()
     expected = 0
-    for axes in phases:
-        count, index = group_of(axes)
-
-        def greet(k, carry, axes=axes, count=count, index=index):
-            pl.semaphore_signal(barrier, inc=1, device_id=peer_id(axes, lax.rem(index + k, count)),
-                                device_id_type=pl.DeviceIdType.MESH)
-            return carry
-
-        each(count, greet)
-        expected = expected + count - 1
-    if len(phases) > 1:
+    if len(phases) == 1:
+        flat = sizes[0] * sizes[1]
+        spot = me[0] * sizes[1] + me[1]
+        for dz in (-1, 0, 1):
+            good = True if dz == 0 else exists((0, 0, dz))
+
+            def greet(k, carry, dz=dz):
+                there = lax.rem(spot + k, flat)
+                pl.semaphore_signal(
+                    barrier, inc=1, device_id_type=pl.DeviceIdType.MESH,
+                    device_id={"gx": lax.div(there, sizes[1]), "gy": lax.rem(there, sizes[1]), "gz": me[2] + dz},
+                )
+                return carry
+
+            if dz == 0:
+                each(flat, greet)
+                expected = expected + flat - 1
+            elif sizes[2] > 1:
+                @pl.when(good)
+                def _():
+                    greet(0, 0)
+                    each(flat, greet)
+                expected = expected + jnp.where(good, flat, 0)
+    else:
+        for axes in phases:
+            count, index = group_of(axes)
+
+            def greet(k, carry, axes=axes, count=count, index=index):
+                pl.semaphore_signal(barrier, inc=1, device_id=peer_id(axes, lax.rem(index + k, count)),
+                                    device_id_type=pl.DeviceIdType.MESH)
+                return carry
+
+            each(count, greet)
+            expected = expected + count - 1
         for direction in directions:
             good = exists(direction)
 
@@ -220,6 +243,21 @@
                 pl.semaphore_signal(barrier, inc=1, device_id=target(direction),
                                     device_id_type=pl.DeviceIdType.MESH)
             expected = expected + jnp.where(good, 1, 0)
+
+    vouches = max(sizes[2] - 2, 0) if len(phases) == 1 else 0
+
+    def vouch(round_):
+        for dz in (-1, 1):
+            @pl.when(exists((0, 0, dz)))
+            def _():
+                pl.semaphore_signal(vouch_sem.at[round_, 0 if dz > 0 else 1], inc=1, device_id=target((0, 0, dz)),
+                                    device_id_type=pl.DeviceIdType.MESH)
+
+    def vouched(round_):
+        for dz in (-1, 1):
+            @pl.when(exists((0, 0, dz)))
+            def _():
+                pl.semaphore_wait(vouch_sem.at[round_, 1 if dz > 0 else 0], 1)
 
     lane = lax.broadcasted_iota(jnp.int32, (1, LANES), 1)
     firsts = lasts = jnp.zeros((2 * cols, LANES), F32)
@@ -238,6 +276,8 @@
     ends[1] = lasts.astype(BF16)
     pl.semaphore_wait(barrier, expected)
     halo_start(0)
+    if vouches:
+        vouch(0)
 
     def block_of(x, y):
         bx, lx = (0, nx - 1) if x == 0 else (2, 0) if x == nx + 1 else (1, x - 1)
@@ -328,9 +368,11 @@
     def image_at2(x, y):
         return stack2[x, y, cols:, :]
 
-    sum_start(0, 0, pack(gram(loads_at, loads_at)))
+    load_part = pack(gram(loads_at, loads_at))
+    for round_ in range(1, vouches):
+        vouched(round_ - 1)
+        vouch(round_)
     halo_arrive(0)
-    sum_turn(0)
     full = nz + LANES
     moduli = {}
     for x in xs:
@@ -351,6 +393,11 @@
             weight = 0.125 * (total + pltpu.roll(total, full - 1, 1))
             wt[x, y] = weight
             wtr[x, y] = pltpu.roll(weight, 1, 1)
+
+    if vouches:
+        vouched(vouches - 1)
+    sum_start(0, 0, load_part)
+    sum_turn(0)
 
     def double(tile):
         return jnp.concatenate([tile, tile], axis=0)
@@ -467,7 +514,7 @@
     phases = (AXES,) if count <= DIRECT_LIMIT else (("gx", "gy"), ("gz",))
     slots = sum(int(np.prod([sizes[AXES.index(a)] for a in axes])) for axes in phases)
     body = functools.partial(kernel_body, sizes, phases, stiffness_values())
-    out = jax.ShapeDtypeStruct((cols, nx, ny, nz), F32)
+    out = pltpu.VMEM((cols, nx, ny, nz), F32)
     vmem = pl.BlockSpec(memory_space=pltpu.VMEM)
     anywhere = pl.BlockSpec(memory_space=pl.ANY)
     full = nz + LANES
@@ -498,6 +545,7 @@
             pltpu.SemaphoreType.DMA((3, slots)),
             pltpu.VMEM((2, nx, ny, cols, nz), F32),
             pltpu.SemaphoreType.DMA((3, nx * ny)),
+            pltpu.SemaphoreType.REGULAR((max(sizes[2], 2), 2)),
         ],
         compiler_params=pltpu.CompilerParams(collective_id=0, has_side_effects=True),
     )(moduli, loads, material)

time: 37.6 us -> 35.3 us (0.939)
  Pallas kernels: 34.5 us -> 33.1 us
  local copies, waits for them, and re-layouts: 2.26 us -> 1.31 us
    pallas_call x1, Pallas kernels: 34.5 us -> 33.1 us  [on_device(): pl.pallas_call(body, out_shape=(out, out), in_specs=[pl.BlockSpec(memory_...]
    unnamed x4 -> x2, local copies, waits for them, and re-layouts: 2.26 us -> 1.31 us
where the time goes in v4:
time: 35.3 us; the launch traced here: 35 us
  Pallas kernels  33.1 us (94%)
  local copies, waits for them, and re-layouts  1.31 us (4%)
  between operations  0.64 us (2%)
    pallas_call x1, Pallas kernels, on_device(): pl.pallas_call(body, out_shape=(out, out), in_specs=[pl.BlockSpec(memory_...  33.1 us
    unnamed x2, local copies, waits for them, and re-layouts  1.31 us

profile of v4, /device:TPU:0, one launch (start us, length us, event | category | flops | bytes accessed | tf_op | source)
XLA Modules:
  0.0 35.0 jit_solution(17384715966097938411)
XLA Ops:
  0.6 33.1 %shard_map.50 = (f32[16,2,4,256]{3,2,1,0:T(4,128)S(1)}, f32[16,2,4,256]{3,2,1,0:T(4,128)S(1)}) custom-call(f32[8]{0:T(128)} %moduli_ref.1, f32[16,2,4,256]{3,2,1,0:T(4,128)} %loads_ref.1, s32[2,4,256]{2,1,0:T(4,128)} %mat_ref.1), custom_call_target="tpu_custom_call" | custom-call | tf_op jit(solution)/shard_map/pallas_call | solution.py:521
  33.7 0.7 %copy.7 = f32[16,2,4,256]{3,2,1,0:T(4,128)} copy(f32[16,2,4,256]{3,2,1,0:T(4,128)S(1)} %get-tuple-element.2) | data formatting | bytes 262144
  34.4 0.7 %copy.8 = f32[16,2,4,256]{3,2,1,0:T(4,128)} copy(f32[16,2,4,256]{3,2,1,0:T(4,128)S(1)} %get-tuple-element.3) | data formatting | bytes 262144
